TPU v7x, 32 devices: a whole 2x2x4 slice. The times are simulated.
32 devices in a mesh: gx: 8 (over y, x, core), gy: 4 (over z).
Axes of the slice: x: 2, y: 2, z: 4, core: 2. Of those that a mesh axis runs over, the one named last changes fastest.
Arguments:
- queries: bfloat16 [512, 2048], P(('gx', 'gy')), may hold values from -6 to 6
- probe_dev: int32 [512, 16], P(('gx', 'gy')), may hold values from 0 to 31, all different within a row; in each aligned block of 16 rows (0 to 15, 16 to 31, ...) at most 10 rows name the same one
- probe_list: int32 [512, 16], P(('gx', 'gy')), may hold values from 0 to 15
- documents: bfloat16 [512, 256, 2048], P(('gx', 'gy')), may hold values from -6 to 6
- lengths: int32 [512], P(('gx', 'gy')), may hold values from 96 to 256, as said below
- short_dev: int32 [512, 32], P(('gx', 'gy')), may hold values from 0 to 31, all different within a row; in each aligned block of 16 rows (0 to 15, 16 to 31, ...) at most 16 rows name the same one
- short_list: int32 [512, 32], P(('gx', 'gy')), may hold values from 0 to 15
- short_row: int32 [512, 32], P(('gx', 'gy')), may hold values from 0 to 95
Outputs:
- prefix_top: float32 [512, 32], P(('gx', 'gy'))
- rescored: float32 [512, 32], P(('gx', 'gy'))
Inputs may be any that keep to these rules, and one draw needn't show every extreme that they name: `lengths`: every list holds at least 96 documents, and in every draw some list is full. `probe_dev`: the 16 entries of a query name different devices. Among the 16 queries of one device, no device is named more than 10 times, and some device is named exactly 10 times. `short_dev`: the 32 entries of a query name different devices. Among the 16 queries of one device, no device is named more than 16 times, and some device is named exactly 16 times.
All inputs are finite; a program needn't handle non-finite values.
Results may differ from a plain program's by a relative error of at most 0.0029.
Values may be sent and summed in bfloat16 or wider, within the bound.
A program may use at most 128 MiB of HBM per device.

v0:
```python
import jax
import jax.numpy as jnp
from jax import lax
from jax.sharding import PartitionSpec as P

PREFIX = 256
TOPK = 32


def unit_rows(values):
    return values / jnp.sqrt(1.0 + jnp.sum(values * values, axis=1, keepdims=True))


def top_values(values, count):
    return -jnp.sort(-values, axis=-1)[..., :count]


def slot_numbers(targets, count_dev):
    onehot = (targets[:, None] == jnp.arange(count_dev, dtype=jnp.int32)[None, :]).astype(jnp.int32)
    return jnp.sum(onehot * (jnp.cumsum(onehot, axis=0) - 1), axis=1)


def place_codes(position, total, codes):
    hits = position[:, None] == jnp.arange(total, dtype=jnp.int32)[None, :]
    return jnp.sum(jnp.where(hits, codes[:, None], 0), axis=0)


def place_vectors(position, total, vectors):
    hits = (position[:, None] == jnp.arange(total, dtype=jnp.int32)[None, :]).astype(jnp.bfloat16)
    placed = lax.dot_general(
        hits, vectors, (((0,), (0,)), ((), ())), preferred_element_type=jnp.float32
    )
    return placed.astype(jnp.bfloat16)


def prefix_scores(rows, documents, width):
    scores = lax.dot_general(
        rows, documents[:, :, :width], (((1,), (2,)), ((), ())), preferred_element_type=jnp.float32
    )
    return scores.reshape(rows.shape[0], -1)


def shards(queries, probe_dev, probe_list, documents, lengths, short_dev, short_list, short_row):
    query_float = queries.astype(jnp.float32)
    prefix_unit = unit_rows(query_float[:, :PREFIX]).astype(jnp.bfloat16)
    full_unit = unit_rows(query_float).astype(jnp.bfloat16)
    local_lists = documents.shape[0]
    rows_list = documents.shape[1]
    count_dev = lax.axis_size(("gx", "gy"))
    query_rows = queries.shape[0]
    probe_count = probe_dev.shape[1]
    pair_cap = min(query_rows, max(1, 4 * query_rows * probe_count // (3 * count_dev)))
    pair_dev = probe_dev.reshape(-1)
    pair_slot = slot_numbers(pair_dev, count_dev)
    pair_flat = pair_dev * pair_cap + pair_slot
    pair_prefix = jnp.repeat(prefix_unit, probe_count, axis=0)
    send_prefix = place_vectors(pair_flat, count_dev * pair_cap, pair_prefix).reshape(
        count_dev, pair_cap, PREFIX
    )
    send_list = (
        place_codes(pair_flat, count_dev * pair_cap, probe_list.reshape(-1))
        .astype(jnp.bfloat16)
        .reshape(count_dev, pair_cap)
    )
    got_prefix = lax.all_to_all(send_prefix, ("gx", "gy"), split_axis=0, concat_axis=0, tiled=True)
    got_list = lax.all_to_all(send_list, ("gx", "gy"), split_axis=0, concat_axis=0, tiled=True)
    senders = got_prefix.shape[0]
    items = got_prefix.shape[1]
    flat = got_prefix.reshape(senders * items, PREFIX)
    scores = prefix_scores(flat, documents, PREFIX).reshape(senders * items, local_lists, rows_list)
    which = (
        got_list.reshape(-1).astype(jnp.int32)[:, None]
        == jnp.arange(local_lists, dtype=jnp.int32)[None, :]
    )
    chosen = jnp.sum(jnp.where(which[:, :, None], scores, 0.0), axis=1)
    list_len = jnp.sum(jnp.where(which, lengths[None, :], 0), axis=1)
    keep_mask = jnp.arange(rows_list)[None, :] < list_len[:, None]
    best = top_values(jnp.where(keep_mask, chosen, -jnp.inf), TOPK).reshape(senders, items, TOPK)
    returned = lax.all_to_all(best, ("gx", "gy"), split_axis=0, concat_axis=0, tiled=True)
    pooled = returned.reshape(count_dev * pair_cap, TOPK)[pair_flat].reshape(
        query_rows, probe_count * TOPK
    )
    prefix_top = top_values(pooled, TOPK)
    shortlist = short_dev.shape[1]
    capacity = min(query_rows, max(1, 4 * query_rows * shortlist // (3 * count_dev)))
    targets = short_dev.reshape(-1)
    request_codes = (short_list * rows_list + short_row).reshape(-1)
    slot_ids = slot_numbers(targets, count_dev)
    flat_slots = targets * capacity + slot_ids
    requests = place_codes(flat_slots, count_dev * capacity, request_codes).reshape(
        count_dev, capacity
    )
    doc_table = documents.reshape(local_lists * rows_list, documents.shape[2])
    found_rows = doc_table[
        lax.all_to_all(requests, ("gx", "gy"), split_axis=0, concat_axis=0, tiled=True)
    ]
    fetched = lax.all_to_all(found_rows, ("gx", "gy"), split_axis=0, concat_axis=0, tiled=True)
    vectors = fetched.reshape(count_dev * capacity, -1)[flat_slots].reshape(
        query_rows, shortlist, -1
    )
    rescored = jnp.einsum("qsf,qf->qs", vectors, full_unit, preferred_element_type=jnp.float32)
    return (prefix_top, rescored)


def solution(mesh):
    in_specs = (
        P(("gx", "gy"), None),
        P(("gx", "gy"), None),
        P(("gx", "gy"), None),
        P(("gx", "gy"), None, None),
        P(("gx", "gy")),
        P(("gx", "gy"), None),
        P(("gx", "gy"), None),
        P(("gx", "gy"), None),
    )
    out_specs = (P(("gx", "gy"), None), P(("gx", "gy"), None))
    return jax.shard_map(shards, mesh=mesh, in_specs=in_specs, out_specs=out_specs, check_vma=False)
```

profile of v0, /device:TPU:0, one launch (start us, length us, event | category | flops | bytes accessed | tf_op | source)
XLA Modules:
  0.0 144.3 jit_solution(12532673178704320118)
XLA Ops:
  0.6 0.8 eq.115
  1.4 0.8 reshape.232
  2.2 0.6 reduce-window.14
  3.1 0.8 broadcast_in_dim.78
  4.1 0.7 convert_element_type.58
  4.8 7.3 %all-to-all-start = ((bf16[32,1,10]{2,1,0:T(2,128)(2,1)}), bf16[32,1,10]{2,1,0:T(2,128)(2,1)S(1)}, u32[]{:S(2)}, u32[]{:S(2)}) async-start(bf16[32,1,10]{2,1,0:T(2,128)(2,1)} %convert_element_type.58), calls=%async_computation | async-start | bytes 32768 | tf_op jit(solution)/shard_map/all_to_all | solution.py:66
  12.1 0.8 eq.128
  12.9 0.8 reshape.240
  13.7 0.8 convert_element_type.52
  15.0 1.2 reduce-window.16
  16.6 0.7 multiply_add_fusion
  17.6 0.8 reshape.235
  18.3 0.7 all_to_all.24
  19.0 0.3 all-to-all-done
  19.3 5.5 %all-to-all-start.3 = ((s32[32,1,16]{2,1,0:T(1,128)}), s32[32,1,16]{2,1,0:T(1,128)S(1)}, u32[]{:S(2)}, u32[]{:S(2)}) async-start(s32[32,1,16]{2,1,0:T(1,128)} %bitcast.6), calls=%async_computation.3 | async-start | bytes 32768 | tf_op jit(solution)/shard_map/all_to_all | solution.py:95
  25.0 7.0 %all-to-all-done.3 = s32[32,1,16]{2,1,0:T(1,128)S(1)} async-done(((s32[32,1,16]{2,1,0:T(1,128)}), s32[32,1,16]{2,1,0:T(1,128)S(1)}, u32[]{:S(2)}, u32[]{:S(2)}) %all-to-all-start.3) | async-done | bytes 2080 | tf_op jit(solution)/shard_map/all_to_all | solution.py:95
  32.0 2.6 %all-to-all-start.1 = ((bf16[32,10,256]{2,1,0:T(8,128)(2,1)}), bf16[32,10,256]{2,1,0:T(8,128)(2,1)S(1)}, u32[]{:S(2)}, u32[]{:S(2)}) async-start(bf16[32,10,256]{2,1,0:T(8,128)(2,1)} %reshape.235), calls=%async_computation.1 | async-start | bytes 524288 | tf_op jit(solution)/shard_map/all_to_all | solution.py:65
  34.8 10.0 %all-to-all-done.1 = bf16[32,10,256]{2,1,0:T(8,128)(2,1)S(1)} async-done(((bf16[32,10,256]{2,1,0:T(8,128)(2,1)}), bf16[32,10,256]{2,1,0:T(8,128)(2,1)S(1)}, u32[]{:S(2)}, u32[]{:S(2)}) %all-to-all-start.1) | async-done | bytes 163872 | tf_op jit(solution)/shard_map/all_to_all | solution.py:65
  44.9 2.4 %select_reduce_fusion = f32[320,256]{1,0:T(8,128)S(1)} fusion(pred[320,16]{0,1:T(8,128)(4,1)S(1)} %iota_compare_fusion.8, bf16[320,256,1]{1,0,2:T(8,128)(2,1)S(1)} %reshape.270, bf16[16,256,2048]{2,1,0:T(8,128)(2,1)} %param.11), kind=kOutput, calls=%fused_computation.3 | convolution fusion | flops 673628160 | bytes 2593792 | tf_op jit(solution)/shard_map/dot_general | solution.py:37
  47.4 21.2 %sort_prefixfusion = f32[320,32]{1,0:T(8,128)S(1)} fusion(f32[320,256]{1,0:T(8,128)S(1)} %select_negate_fusion), kind=kCustom, calls=%sort.30.sort_prefix | custom fusion | flops 1392640 | bytes 368640 | tf_op jit(solution)/shard_map/jit(sort)/sort | solution.py:15
  68.7 0.8 reshape.283
  69.5 2.8 %all-to-all-start.2 = ((f32[32,1,320]{2,1,0:T(1,128)}), f32[32,1,320]{2,1,0:T(1,128)S(1)}, u32[]{:S(2)}, u32[]{:S(2)}) async-start(f32[32,1,320]{2,1,0:T(1,128)} %reshape.283), calls=%async_computation.2 | async-start | bytes 98304 | tf_op jit(solution)/shard_map/all_to_all | solution.py:79
  72.3 13.2 %gather_fusion.1 = bf16[512,2048]{1,0:T(8,128)(2,1)} fusion(bf16[4096,2048]{1,0:T(8,128)(2,1)} %bitcast.51, s32[1024]{0:T(1024)S(1)} %pad_clamp_fusion.1), kind=kCustom, calls=%fused_computation.1 | custom fusion | bytes 4196352 | tf_op jit(solution)/shard_map/gather | solution.py:94
  85.5 5.7 %all-to-all-start.4 = ((bf16[32,16,2048]{2,1,0:T(8,128)(2,1)}), bf16[32,16,2048]{2,1,0:T(8,128)(2,1)S(1)}, u32[]{:S(2)}, u32[]{:S(2)}) async-start(bf16[32,16,2048]{2,1,0:T(8,128)(2,1)} %bitcast.52), calls=%async_computation.4 | async-start | bytes 4194304 | tf_op jit(solution)/shard_map/all_to_all | solution.py:97
  91.7 0.5 broadcast.178
  92.2 0.8 reduce.8
  93.1 0.7 gather_fusion
  94.0 3.3 %sort_prefixfusion.1 = f32[16,32]{1,0:T(8,128)S(1)} fusion(f32[16,512]{1,0:T(8,128)S(1)} %neg.18), kind=kCustom, calls=%sort.31.sort_prefix | custom fusion | flops 106496 | bytes 34816 | tf_op jit(solution)/shard_map/jit(sort)/sort | solution.py:15
  97.3 0.6 neg.19
  97.9 40.2 %all-to-all-done.4 = bf16[32,16,2048]{2,1,0:T(8,128)(2,1)S(1)} async-done(((bf16[32,16,2048]{2,1,0:T(8,128)(2,1)}), bf16[32,16,2048]{2,1,0:T(8,128)(2,1)S(1)}, u32[]{:S(2)}, u32[]{:S(2)}) %all-to-all-start.4) | async-done | bytes 2097184 | tf_op jit(solution)/shard_map/all_to_all | solution.py:97
  138.1 3.3 %gather_fusion.2 = bf16[512,2048]{1,0:T(8,128)(2,1)} fusion(bf16[512,2048]{1,0:T(8,128)(2,1)S(1)} %bitcast.50, s32[1024]{0:T(1024)S(1)} %pad_clamp_fusion), kind=kCustom, calls=%fused_computation.2 | custom fusion | bytes 4196352 | tf_op jit(solution)/shard_map/gather | solution.py:98
  141.5 2.8 %fusion.2 = f32[16,1,32]{2,1,0:T(1,128)} fusion(bf16[16,32,2048]{2,1,0:T(8,128)(2,1)} %bitcast.53, bf16[16,2048,1]{1,0,2:T(8,128)(2,1)S(1)} %fusion.6), kind=kOutput, calls=%fused_computation.13 | convolution fusion | flops 2097152 | bytes 2164736 | tf_op jit(solution)/shard_map/qsf,qf->qs/dot_general | solution.py:101
  (56 shorter events, 2.8 us)
Async XLA Ops:
  0.6 34.0 %copy-start.3 = (s32[16]{0:T(128)S(1)}, s32[16]{0:T(128)}, u32[]{:S(2)}) copy-start(s32[16]{0:T(128)} %param.12) | copy-start | bytes 196
  4.8 14.5 %all-to-all-start = ((bf16[32,1,10]{2,1,0:T(2,128)(2,1)}), bf16[32,1,10]{2,1,0:T(2,128)(2,1)S(1)}, u32[]{:S(2)}, u32[]{:S(2)}) async-start(bf16[32,1,10]{2,1,0:T(2,128)(2,1)} %convert_element_type.58), calls=%async_computation | async-start | bytes 32768 | tf_op jit(solution)/shard_map/all_to_all | solution.py:66
  19.3 12.7 %all-to-all-start.3 = ((s32[32,1,16]{2,1,0:T(1,128)}), s32[32,1,16]{2,1,0:T(1,128)S(1)}, u32[]{:S(2)}, u32[]{:S(2)}) async-start(s32[32,1,16]{2,1,0:T(1,128)} %bitcast.6), calls=%async_computation.3 | async-start | bytes 32768 | tf_op jit(solution)/shard_map/all_to_all | solution.py:95
  32.0 12.8 %all-to-all-start.1 = ((bf16[32,10,256]{2,1,0:T(8,128)(2,1)}), bf16[32,10,256]{2,1,0:T(8,128)(2,1)S(1)}, u32[]{:S(2)}, u32[]{:S(2)}) async-start(bf16[32,10,256]{2,1,0:T(8,128)(2,1)} %reshape.235), calls=%async_computation.1 | async-start | bytes 524288 | tf_op jit(solution)/shard_map/all_to_all | solution.py:65
  69.5 16.1 %all-to-all-start.2 = ((f32[32,1,320]{2,1,0:T(1,128)}), f32[32,1,320]{2,1,0:T(1,128)S(1)}, u32[]{:S(2)}, u32[]{:S(2)}) async-start(f32[32,1,320]{2,1,0:T(1,128)} %reshape.283), calls=%async_computation.2 | async-start | bytes 98304 | tf_op jit(solution)/shard_map/all_to_all | solution.py:79
  85.5 5.7 %copy-start.2 = (s32[16,16]{1,0:T(8,128)S(1)}, s32[16,16]{1,0:T(8,128)}, u32[]{:S(2)}) copy-start(s32[16,16]{1,0:T(8,128)} %param.9) | copy-start | bytes 3076
  85.5 5.8 %copy-start.1 = (s32[16,32]{1,0:T(8,128)S(1)}, s32[16,32]{1,0:T(8,128)}, u32[]{:S(2)}) copy-start(s32[16,32]{1,0:T(8,128)} %param.13) | copy-start | bytes 6148
  85.5 5.9 %copy-start = (bf16[16,2048]{1,0:T(8,128)(2,1)S(1)}, bf16[16,2048]{1,0:T(8,128)(2,1)}, u32[]{:S(2)}) copy-start(bf16[16,2048]{1,0:T(8,128)(2,1)} %param.8) | copy-start | bytes 196612
  85.5 52.6 %all-to-all-start.4 = ((bf16[32,16,2048]{2,1,0:T(8,128)(2,1)}), bf16[32,16,2048]{2,1,0:T(8,128)(2,1)S(1)}, u32[]{:S(2)}, u32[]{:S(2)}) async-start(bf16[32,16,2048]{2,1,0:T(8,128)(2,1)} %bitcast.52), calls=%async_computation.4 | async-start | bytes 4194304 | tf_op jit(solution)/shard_map/all_to_all | solution.py:97
where the time goes:
time: 146 us; the launch traced here: 144 us
  waiting for transfers between devices  57.6 us (39%)
  other arithmetic  30.7 us (21%)
  local copies, waits for them, and re-layouts  25.8 us (18%)
  starting transfers between devices  23.9 us (16%)
  matrix products  5.43 us (4%)
    all_to_all x1, waiting for transfers between devices, shards(): lax.all_to_all(found_rows, ('gx', 'gy'), split_axis=0, concat_axis=0, til...  40.2 us
    sort x2, other arithmetic, top_values(): return -jnp.sort(-values, axis=-1)[..., :count]  24.6 us
    gather x1, local copies, waits for them, and re-layouts, shards(): doc_table[lax.all_to_all(requests, ('gx', 'gy'), split_axis=0, concat_axi...  13.2 us
    all_to_all x1, waiting for transfers between devices, shards(): lax.all_to_all(send_prefix, ('gx', 'gy'), split_axis=0, concat_axis=0, ti...  10 us
    all_to_all x1, starting transfers between devices, shards(): lax.all_to_all(send_list, ('gx', 'gy'), split_axis=0, concat_axis=0, tile...  7.33 us
    all_to_all x1, waiting for transfers between devices, shards(): lax.all_to_all(requests, ('gx', 'gy'), split_axis=0, concat_axis=0, tiled...  7.02 us
    all_to_all x1, starting transfers between devices, shards(): lax.all_to_all(found_rows, ('gx', 'gy'), split_axis=0, concat_axis=0, til...  5.67 us
    all_to_all x1, starting transfers between devices, shards(): lax.all_to_all(requests, ('gx', 'gy'), split_axis=0, concat_axis=0, tiled...  5.51 us
  transfers between devices with their start and end apart: 5, of which 4 were waited for; matrix products, arithmetic and copies ran while one was open for 18% of the time, Pallas kernels for 0%

commit v1 on v0

v1 whole, which is shorter than its diff:
```python
import functools

import jax
import jax.numpy as jnp
from jax import lax
from jax.experimental import pallas as pl
from jax.experimental.pallas import tpu as pltpu
from jax.sharding import PartitionSpec as P

PREFIX = 256
TOPK = 32
SHORT_ROWS = 96
AXES = ("gx", "gy")
LANES = 128
HALF = 64
NT = (((1,), (1,)), ((), ()))


def unit_rows(values):
    return values / jnp.sqrt(1.0 + jnp.sum(values * values, axis=1, keepdims=True))


def sort_pairs(n):
    p = 1
    while p < n:
        k = p
        while k >= 1:
            for j in range(k % p, n - k, 2 * k):
                for i in range(min(k, n - j - k)):
                    if (i + j) // (2 * p) == (i + j + k) // (2 * p):
                        yield i + j, i + j + k
            k //= 2
        p *= 2


def sort_desc(v):
    v = list(v)
    for a, b in sort_pairs(len(v)):
        v[a], v[b] = jnp.maximum(v[a], v[b]), jnp.minimum(v[a], v[b])
    return v


def merge_top(a, b):
    n = len(a)
    v = [jnp.maximum(a[i], b[n - 1 - i]) for i in range(n)]
    step = n // 2
    while step:
        for i in range(n):
            if not i & step:
                v[i], v[i + step] = jnp.maximum(v[i], v[i + step]), jnp.minimum(v[i], v[i + step])
        step //= 2
    return v


def score_kernel(probes, shorts, all_ref, len_ref, docs_ref, out_ref, pre_docs, top_docs, chosen, result, sems):
    lists, rows, full = docs_ref.shape
    total = all_ref.shape[0]
    per_dev = 16
    me = (lax.axis_index("gx") * lax.axis_size("gy") + lax.axis_index("gy")).astype(jnp.float32)
    pre_copy = pltpu.make_async_copy(docs_ref.at[:, :, pl.ds(0, PREFIX)], pre_docs, sems.at[0])
    top_copy = pltpu.make_async_copy(docs_ref.at[:, pl.ds(0, SHORT_ROWS), :], top_docs, sems.at[1])
    pre_copy.start()
    top_copy.start()
    pre_copy.wait()
    top_copy.wait()
    tile = chosen.shape[1]
    chunk = 32
    group = 4
    result[...] = jnp.zeros_like(result)

    @pl.loop(0, total // tile)
    def _(block):
        mine = pl.ds(pl.multiple_of(block * tile, tile), tile)
        codes = jnp.transpose(all_ref[mine, full + PREFIX:].astype(jnp.float32))
        p_dev, p_list = codes[:probes], codes[probes:2 * probes]
        base = 2 * probes
        s_dev, s_list, s_row = (codes[base + i * shorts:base + (i + 1) * shorts] for i in range(3))
        probed = jnp.sum(jnp.where(p_dev == me, p_list + 1.0, 0.0), axis=0, keepdims=True).astype(jnp.int32) - 1
        wanted = jnp.sum(jnp.where(s_dev == me, s_list * rows + s_row + 1.0, 0.0), axis=0, keepdims=True).astype(jnp.int32) - 1

        @pl.loop(0, rows // chunk)
        def _(c):
            first = pl.multiple_of(c * chunk, chunk)
            docs = pre_docs[:, pl.ds(first, chunk), :].reshape(lists * chunk, PREFIX)
            scores = lax.dot_general(docs, all_ref[mine, full:full + PREFIX], NT, preferred_element_type=jnp.float32)
            slot = lax.broadcasted_iota(jnp.int32, (chunk, tile), 0) + first
            value = jnp.full((chunk, tile), -jnp.inf, jnp.float32)
            for l in range(lists):
                limit = jnp.where(probed == l, len_ref[l], 0)
                value = jnp.where(slot < limit, scores[l * chunk:(l + 1) * chunk], value)
            chosen[pl.ds(first, chunk), :] = value

        @pl.loop(0, tile // LANES)
        def _(t):
            lanes = pl.ds(pl.multiple_of(t * LANES, LANES), LANES)
            v = [chosen[pl.ds(8 * i, 8), lanes] for i in range(rows // 8)]
            parts = [sort_desc(v[i:i + TOPK]) for i in range(0, len(v), TOPK)]
            v = functools.reduce(merge_top, parts)
            for shift in (4, 2, 1):
                v = merge_top(v, [pltpu.roll(x, shift, 0) for x in v])
            sub = lax.broadcasted_iota(jnp.int32, (8, LANES), 0)
            for a in range(TOPK // 8):
                packed = v[8 * a]
                for s in range(1, 8):
                    packed = jnp.where(sub == s, v[8 * a + s], packed)
                result[pl.ds(8 * a, 8), lanes] = packed

        def rescore(g, acc):
            docs = top_docs[pl.ds(g * group, group)].reshape(group * SHORT_ROWS, full)
            scores = lax.dot_general(docs, all_ref[mine, :full], NT, preferred_element_type=jnp.float32)
            slot = lax.broadcasted_iota(jnp.int32, (SHORT_ROWS, tile), 0)
            for j in range(group):
                hit = slot == wanted - (g * group + j) * rows
                part = jnp.where(hit, scores[j * SHORT_ROWS:(j + 1) * SHORT_ROWS], 0.0)
                acc = acc + jnp.sum(part.reshape(SHORT_ROWS // 8, 8, tile), axis=0)
            return acc

        acc = lax.fori_loop(0, lists // group, rescore, jnp.zeros((8, tile), jnp.float32))
        result[TOPK:TOPK + 8, :] = jnp.broadcast_to(jnp.sum(acc, axis=0, keepdims=True), (8, tile))
        lane = lax.broadcasted_iota(jnp.int32, (8, LANES), 1)
        for t in range(tile // LANES):
            turned = jnp.transpose(result[:, t * LANES:(t + 1) * LANES])
            for d in range(LANES // per_dev):
                low = turned[d * per_dev:d * per_dev + 8]
                high = pltpu.roll(turned[d * per_dev + 8:(d + 1) * per_dev], HALF, 1)
                out_ref[block * (tile // per_dev) + t * (LANES // per_dev) + d] = jnp.where(lane < HALF, low, high)


def merge_kernel(got_ref, dev_ref, top_ref, short_ref):
    count = got_ref.shape[0]
    shorts = dev_ref.shape[1]
    v = [got_ref[i] for i in range(count)]
    pad = -count % TOPK
    v = v + [jnp.full_like(v[0], -jnp.inf)] * pad
    parts = [sort_desc(v[i:i + TOPK]) for i in range(0, len(v), TOPK)]
    best = functools.reduce(merge_top, parts)
    shift = TOPK // 2
    while shift:
        best = merge_top(best, [pltpu.roll(x, LANES - shift, 1) for x in best])
        shift //= 2
    lane = lax.broadcasted_iota(jnp.int32, (8, LANES), 1)
    out = best[0]
    for i in range(1, TOPK):
        out = jnp.where(lane % HALF == i, pltpu.roll(best[i], i, 1), out)
    top_ref[0:8, :] = out[:, :TOPK]
    top_ref[8:16, :] = pltpu.roll(out, HALF, 1)[:, :TOPK]
    for h in range(2):
        dev = dev_ref[8 * h:8 * h + 8, :]
        acc = jnp.zeros((8, shorts), jnp.float32)
        for i in range(count):
            spot = HALF * h + TOPK
            acc = jnp.where(dev == i, jnp.broadcast_to(got_ref[i][:, spot:spot + 1], (8, shorts)), acc)
        short_ref[8 * h:8 * h + 8, :] = acc


def shards(queries, probe_dev, probe_list, documents, lengths, short_dev, short_list, short_row):
    count = lax.axis_size(AXES)
    lists, rows, full = documents.shape
    query_rows = queries.shape[0]
    probes, shorts = probe_dev.shape[1], short_dev.shape[1]
    query_float = queries.astype(jnp.float32)
    codes = jnp.concatenate([probe_dev, probe_list, short_dev, short_list, short_row], axis=1)
    packed = jnp.concatenate([
        unit_rows(query_float).astype(jnp.bfloat16),
        unit_rows(query_float[:, :PREFIX]).astype(jnp.bfloat16),
        codes.astype(jnp.bfloat16),
    ], axis=1)
    everyone = lax.all_gather(packed, AXES, axis=0, tiled=True)
    total = count * query_rows
    tile = min(512, total)
    vmem = pl.BlockSpec(memory_space=pltpu.VMEM)
    returned = pl.pallas_call(
        functools.partial(score_kernel, probes, shorts),
        out_shape=jax.ShapeDtypeStruct((count, 8, LANES), jnp.float32),
        in_specs=[vmem, pl.BlockSpec(memory_space=pltpu.SMEM), pl.BlockSpec(memory_space=pl.ANY)],
        out_specs=vmem,
        scratch_shapes=[
            pltpu.VMEM((lists, rows, PREFIX), jnp.bfloat16),
            pltpu.VMEM((lists, SHORT_ROWS, full), jnp.bfloat16),
            pltpu.VMEM((rows, tile), jnp.float32),
            pltpu.VMEM((LANES, tile), jnp.float32),
            pltpu.SemaphoreType.DMA((2,)),
        ],
        compiler_params=pltpu.CompilerParams(vmem_limit_bytes=60 * 1024 * 1024),
        name="score",
    )(everyone, lengths, documents)
    got = lax.all_to_all(returned, AXES, split_axis=0, concat_axis=0, tiled=True)
    return pl.pallas_call(
        merge_kernel,
        out_shape=(
            jax.ShapeDtypeStruct((query_rows, TOPK), jnp.float32),
            jax.ShapeDtypeStruct((query_rows, shorts), jnp.float32),
        ),
        in_specs=[vmem, vmem],
        out_specs=(vmem, vmem),
        name="merge",
    )(got, short_dev)


def solution(mesh):
    one = P(AXES, None)
    in_specs = (one, one, one, P(AXES, None, None), P(AXES), one, one, one)
    return jax.shard_map(shards, mesh=mesh, in_specs=in_specs, out_specs=(one, one), check_vma=False)
```

time: 146 us -> 110 us (0.75)
  local copies, waits for them, and re-layouts: 25.8 us -> 0.72 us
  other arithmetic: 30.7 us -> 6.45 us
  starting transfers between devices: 23.9 us -> 0.04 us
  Pallas kernels: 0 us -> 15.7 us
  between operations: 0.91 us -> 14.1 us
  blocking collectives: 0 us -> 11.9 us
  matrix products: 5.43 us -> 0 us
  waiting for transfers between devices: 57.6 us -> 60.2 us
    all_gather x0 -> x1, waiting for transfers between devices: none -> 60.2 us  [shards(): everyone = lax.all_gather(packed, AXES, axis=0, tiled=True)]
    all_to_all x5 -> x0, waiting for transfers between devices: 57.6 us -> none  [the longest x1 40.2 us: shards(): lax.all_to_all(found_rows, ('gx', 'gy'), split_axis=0, concat_axis=0, til...]
    sort x2 -> x0, other arithmetic: 24.6 us -> none  [top_values(): return -jnp.sort(-values, axis=-1)[..., :count]]
    all_to_all x5 -> x0, starting transfers between devices: 23.9 us -> none  [the longest x1 7.33 us: shards(): lax.all_to_all(send_list, ('gx', 'gy'), split_axis=0, concat_axis=0, tile...]
    gather x3 -> x0, local copies, waits for them, and re-layouts: 17.3 us -> none  [the longest x1 13.2 us: shards(): doc_table[lax.all_to_all(requests, ('gx', 'gy'), split_axis=0, concat_axi...]
    pallas_call x0 -> x2, Pallas kernels: none -> 15.7 us  [the longest x1 13.5 us: shards(): pl.pallas_call(functools.partial(score_kernel, probes, shorts), out_shape...]
    all_to_all x0 -> x1, blocking collectives: none -> 11.9 us  [shards(): lax.all_to_all(returned, AXES, split_axis=0, concat_axis=0, tiled=True)]
    dot_general x3 -> x0, matrix products: 5.43 us -> none  [the longest x1 2.84 us: shards(): jnp.einsum('qsf,qf->qs', vectors, full_unit, preferred_element_type=jnp.f...]
  transfers between devices with their start and end apart: 5 -> 1, of which waited for: 4 -> 1; matrix products, arithmetic and copies ran while one was open for 18% -> 0% of each run, Pallas kernels for 0% -> 0%
where the time goes in v1:
time: 110 us; the launch traced here: 109 us
  waiting for transfers between devices  60.2 us (55%)
  Pallas kernels  15.7 us (14%)
  between operations  14.1 us (13%)
  blocking collectives  11.9 us (11%)
  other arithmetic  6.45 us (6%)
    all_gather x1, waiting for transfers between devices, shards(): everyone = lax.all_gather(packed, AXES, axis=0, tiled=True)  60.2 us
    pallas_call x1, Pallas kernels, shards(): pl.pallas_call(functools.partial(score_kernel, probes, shorts), out_shape...  13.5 us
    all_to_all x1, blocking collectives, shards(): lax.all_to_all(returned, AXES, split_axis=0, concat_axis=0, tiled=True)  11.9 us
    another operation x5, other arithmetic  3.5 us
    pallas_call x1, Pallas kernels, shards(): pl.pallas_call(merge_kernel, out_shape=(jax.ShapeDtypeStruct((query_rows,...  2.25 us
  transfers between devices with their start and end apart: 1, of which 1 were waited for; matrix products, arithmetic and copies ran while one was open for 0% of the time, Pallas kernels for 0%

profile of v1, /device:TPU:0, one launch (start us, length us, event | category | flops | bytes accessed | tf_op | source)
XLA Modules:
  0.0 109.1 jit_solution(6292105325203001854)
XLA Ops:
  7.2 0.0 all-gather.2.cloned.1.call-start
  7.2 1.0 multiply_reduce_fusion
  8.2 0.9 convert_element_type.10
  9.0 0.7 convert.15
  9.8 0.7 convert.16
  10.5 0.7 convert.18
  11.2 0.7 convert.19
  11.9 0.7 convert.17
  12.6 0.9 divide_convert_fusion
  13.5 0.1 multiply_reduce_fusion.1
  13.6 0.1 divide_convert_fusion.1
  13.7 0.7 concatenate.6
  14.4 0.0 all-gather.2.cloned.1.call-update
  14.4 60.2 %all-gather.2.cloned.1.call-done.all_ref = bf16[512,2432]{1,0:T(8,128)(2,1)} async-done(((bf16[16,2432]{1,0:T(8,128)(2,1)}), bf16[512,2432]{1,0:T(8,128)(2,1)}) %all-gather.2.cloned.1.call-update) | async-done | bytes 2490384 | tf_op jit(solution)/shard_map/all_gather | solution.py:168
  74.6 13.5 %score.1 = f32[32,8,128]{2,1,0:T(8,128)} custom-call(bf16[512,2432]{1,0:T(8,128)(2,1)} %all-gather.2.cloned.1.call-done.all_ref, s32[16]{0:T(128)} %len_ref.1, bf16[16,256,2048]{2,1,0:T(8,128)(2,1)} %docs_ref.1), custom_call_target="tpu_custom_call" | custom-call | tf_op jit(solution)/shard_map/score/pallas_call | solution.py:172
  88.1 11.9 %all_to_all.5.got_ref = f32[32,8,128]{2,1,0:T(8,128)} all-to-all(f32[32,8,128]{2,1,0:T(8,128)} %score.1), channel_id=1, replica_groups=mesh['gx'=8,'gy'=4] {'gx','gy'}, dimensions={0} | all-to-all | bytes 262144 | tf_op jit(solution)/shard_map/all_to_all | solution.py:187
  100.0 2.2 %merge.1 = (f32[16,32]{1,0:T(8,128)}, f32[16,32]{1,0:T(8,128)}) custom-call(f32[32,8,128]{2,1,0:T(8,128)} %all_to_all.5.got_ref, s32[16,32]{1,0:T(8,128)} %dev_ref.1), custom_call_target="tpu_custom_call" | custom-call | tf_op jit(solution)/shard_map/merge/pallas_call | solution.py:188
  (2 shorter events, 0.0 us)
Async XLA Ops:
  7.2 67.5 %all-gather.2.cloned.1.call-start = ((), (), s32[]{:S(2)}) async-start(), calls=%async_computation.1 | async-start | bytes 2568192 | tf_op jit(solution)/shard_map/all_gather | solution.py:168
Sparse Core Ops, SparseCore 0:
  14.5 60.0 all-gather.1

commit v2 on v1

--- a/solution.py
+++ b/solution.py
@@ -14,6 +14,7 @@
 LANES = 128
 HALF = 64
 NT = (((1,), (1,)), ((), ()))
+MESH = pl.DeviceIdType.MESH
 
 
 def unit_rows(values):
@@ -52,9 +53,126 @@
     return v
 
 
-def score_kernel(probes, shorts, all_ref, len_ref, docs_ref, out_ref, pre_docs, top_docs, chosen, result, sems):
+def device_of(position):
+    size = lax.axis_size("gy")
+    return position // size, position % size
+
+
+def gather_kernel(split, q_ref, code_ref, a_ref, b_ref, line_send, line_recv, cube_send, cube_recv):
+    gx, gy = lax.axis_index("gx"), lax.axis_index("gy")
+    line = lax.axis_size("gy")
+    bits = len(a_ref.shape) - 3
+    outs = (a_ref, b_ref)
+
+    def flip(bit):
+        size = 1 << bit
+        return gx + (1 - 2 * ((gx // size) % 2)) * size
+
+    def view(ref, free, slot):
+        spots = [slice(None) if b in free else (gx // (1 << b)) % 2 for b in range(bits - 1, -1, -1)]
+        return ref.at[tuple(spots) + (slot,)]
+
+    barrier = pltpu.get_barrier_semaphore()
+    for k in range(1, line):
+        pl.semaphore_signal(barrier, inc=1, device_id=(gx, (gy + k) % line), device_id_type=MESH)
+    for b in range(bits):
+        pl.semaphore_signal(barrier, inc=1, device_id=(flip(b), gy), device_id_type=MESH)
+    values = q_ref[...].astype(jnp.float32)
+    unit = unit_rows(values).astype(jnp.bfloat16)
+    view(a_ref, (), gy)[...] = unit[:, :split]
+    rest = unit.shape[1] - split
+    own = view(b_ref, (), gy)
+    own[:, :rest] = unit[:, split:]
+    own[:, rest:rest + PREFIX] = unit_rows(values[:, :PREFIX]).astype(jnp.bfloat16)
+    own[:, rest + PREFIX:] = code_ref[...]
+    pl.semaphore_wait(barrier, line - 1 + bits)
+
+    offsets = sorted(range(1, line), key=lambda k: (min(k, line - k), k))
+
+    def line_copy(piece, k):
+        ref = outs[piece]
+        return pltpu.make_async_remote_copy(
+            src_ref=view(ref, (), gy), dst_ref=view(ref, (), gy),
+            send_sem=line_send.at[piece, k], recv_sem=line_recv.at[piece, k],
+            device_id=(gx, (gy + k) % line), device_id_type=MESH,
+        )
+
+    order = (list(range(1, bits)) + [0], list(range(bits - 1, 0, -1)) + [0])
+
+    def cube_copy(piece, k, step):
+        ref, slot = outs[piece], (gy + line - k) % line
+        src = view(ref, order[piece][:step], slot)
+        return pltpu.make_async_remote_copy(
+            src_ref=src, dst_ref=src,
+            send_sem=cube_send.at[piece, k, step], recv_sem=cube_recv.at[piece, k, step],
+            device_id=(flip(order[piece][step]), gy), device_id_type=MESH,
+        )
+
+    steps = bits
+    slots = [0] + offsets
+    for k in offsets:
+        for piece in range(2):
+            line_copy(piece, k).start()
+    for wave in range(len(slots) + steps):
+        for step in range(steps, -1, -1):
+            if not 0 <= wave - step < len(slots):
+                continue
+            k = slots[wave - step]
+            for piece in range(2):
+                if step == 0 and k:
+                    line_copy(piece, k).wait_recv()
+                if step > 0:
+                    cube_copy(piece, k, step - 1).wait_recv()
+                if step < steps:
+                    cube_copy(piece, k, step).start()
+    for piece in range(2):
+        for k in offsets:
+            line_copy(piece, k).wait_send()
+        for k in slots:
+            for step in range(steps):
+                cube_copy(piece, k, step).wait_send()
+
+
+def exchange_kernel(src_ref, out_ref, send_sem, recv_sem, own_sem):
+    count = src_ref.shape[0]
+    me = lax.axis_index("gx") * lax.axis_size("gy") + lax.axis_index("gy")
+    barrier = pltpu.get_barrier_semaphore()
+
+    @pl.loop(1, count)
+    def _(k):
+        pl.semaphore_signal(barrier, inc=1, device_id=device_of((me + k) % count), device_id_type=MESH)
+
+    own = pltpu.make_async_copy(src_ref.at[me], out_ref.at[me], own_sem)
+    own.start()
+    pl.semaphore_wait(barrier, count - 1)
+
+    def copy(k):
+        peer = (me + k) % count
+        return pltpu.make_async_remote_copy(
+            src_ref=src_ref.at[peer], dst_ref=out_ref.at[me],
+            send_sem=send_sem.at[k], recv_sem=recv_sem.at[k],
+            device_id=device_of(peer), device_id_type=MESH,
+        )
+
+    @pl.loop(1, count)
+    def _(k):
+        copy(k).start()
+
+    own.wait()
+
+    @pl.loop(1, count)
+    def _(k):
+        copy(k).wait_recv()
+
+    @pl.loop(1, count)
+    def _(k):
+        copy(k).wait_send()
+
+
+def score_kernel(probes, shorts, a_ref, b_ref, len_ref, docs_ref, out_ref, pre_docs, top_docs, chosen, result, sems):
     lists, rows, full = docs_ref.shape
-    total = all_ref.shape[0]
+    total, split = a_ref.shape
+    rest = full - split
     per_dev = 16
     me = (lax.axis_index("gx") * lax.axis_size("gy") + lax.axis_index("gy")).astype(jnp.float32)
     pre_copy = pltpu.make_async_copy(docs_ref.at[:, :, pl.ds(0, PREFIX)], pre_docs, sems.at[0])
@@ -71,7 +189,7 @@
     @pl.loop(0, total // tile)
     def _(block):
         mine = pl.ds(pl.multiple_of(block * tile, tile), tile)
-        codes = jnp.transpose(all_ref[mine, full + PREFIX:].astype(jnp.float32))
+        codes = jnp.transpose(b_ref[mine, rest + PREFIX:].astype(jnp.float32))
         p_dev, p_list = codes[:probes], codes[probes:2 * probes]
         base = 2 * probes
         s_dev, s_list, s_row = (codes[base + i * shorts:base + (i + 1) * shorts] for i in range(3))
@@ -82,7 +200,7 @@
         def _(c):
             first = pl.multiple_of(c * chunk, chunk)
             docs = pre_docs[:, pl.ds(first, chunk), :].reshape(lists * chunk, PREFIX)
-            scores = lax.dot_general(docs, all_ref[mine, full:full + PREFIX], NT, preferred_element_type=jnp.float32)
+            scores = lax.dot_general(docs, b_ref[mine, rest:rest + PREFIX], NT, preferred_element_type=jnp.float32)
             slot = lax.broadcasted_iota(jnp.int32, (chunk, tile), 0) + first
             value = jnp.full((chunk, tile), -jnp.inf, jnp.float32)
             for l in range(lists):
@@ -107,7 +225,8 @@
 
         def rescore(g, acc):
             docs = top_docs[pl.ds(g * group, group)].reshape(group * SHORT_ROWS, full)
-            scores = lax.dot_general(docs, all_ref[mine, :full], NT, preferred_element_type=jnp.float32)
+            scores = lax.dot_general(docs[:, :split], a_ref[mine, :], NT, preferred_element_type=jnp.float32)
+            scores = scores + lax.dot_general(docs[:, split:], b_ref[mine, :rest], NT, preferred_element_type=jnp.float32)
             slot = lax.broadcasted_iota(jnp.int32, (SHORT_ROWS, tile), 0)
             for j in range(group):
                 hit = slot == wanted - (g * group + j) * rows
@@ -158,21 +277,35 @@
     lists, rows, full = documents.shape
     query_rows = queries.shape[0]
     probes, shorts = probe_dev.shape[1], short_dev.shape[1]
-    query_float = queries.astype(jnp.float32)
     codes = jnp.concatenate([probe_dev, probe_list, short_dev, short_list, short_row], axis=1)
-    packed = jnp.concatenate([
-        unit_rows(query_float).astype(jnp.bfloat16),
-        unit_rows(query_float[:, :PREFIX]).astype(jnp.bfloat16),
-        codes.astype(jnp.bfloat16),
-    ], axis=1)
-    everyone = lax.all_gather(packed, AXES, axis=0, tiled=True)
+    line = lax.axis_size("gy")
+    bits = (count // line).bit_length() - 1
+    split = (full + PREFIX + LANES + 2 * LANES - 1) // (2 * LANES) * LANES
+    widths = (split, full - split + PREFIX + codes.shape[1])
+    vmem = pl.BlockSpec(memory_space=pltpu.VMEM)
+    everyone = pl.pallas_call(
+        functools.partial(gather_kernel, split),
+        out_shape=tuple(
+            jax.ShapeDtypeStruct((2,) * bits + (line, query_rows, width), jnp.bfloat16) for width in widths
+        ),
+        in_specs=[vmem, vmem],
+        out_specs=(vmem, vmem),
+        scratch_shapes=[
+            pltpu.SemaphoreType.DMA((2, line)),
+            pltpu.SemaphoreType.DMA((2, line)),
+            pltpu.SemaphoreType.DMA((2, line, bits)),
+            pltpu.SemaphoreType.DMA((2, line, bits)),
+        ],
+        compiler_params=pltpu.CompilerParams(collective_id=0, has_side_effects=True),
+        name="gather",
+    )(queries, codes.astype(jnp.bfloat16))
+    everyone = [x.reshape(-1, x.shape[-1]) for x in everyone]
     total = count * query_rows
     tile = min(512, total)
-    vmem = pl.BlockSpec(memory_space=pltpu.VMEM)
     returned = pl.pallas_call(
         functools.partial(score_kernel, probes, shorts),
         out_shape=jax.ShapeDtypeStruct((count, 8, LANES), jnp.float32),
-        in_specs=[vmem, pl.BlockSpec(memory_space=pltpu.SMEM), pl.BlockSpec(memory_space=pl.ANY)],
+        in_specs=[vmem, vmem, pl.BlockSpec(memory_space=pltpu.SMEM), pl.BlockSpec(memory_space=pl.ANY)],
         out_specs=vmem,
         scratch_shapes=[
             pltpu.VMEM((lists, rows, PREFIX), jnp.bfloat16),
@@ -183,8 +316,20 @@
         ],
         compiler_params=pltpu.CompilerParams(vmem_limit_bytes=60 * 1024 * 1024),
         name="score",
-    )(everyone, lengths, documents)
-    got = lax.all_to_all(returned, AXES, split_axis=0, concat_axis=0, tiled=True)
+    )(*everyone, lengths, documents)
+    got = pl.pallas_call(
+        exchange_kernel,
+        out_shape=jax.ShapeDtypeStruct(returned.shape, returned.dtype),
+        in_specs=[vmem],
+        out_specs=vmem,
+        scratch_shapes=[
+            pltpu.SemaphoreType.DMA((count,)),
+            pltpu.SemaphoreType.DMA((count,)),
+            pltpu.SemaphoreType.DMA,
+        ],
+        compiler_params=pltpu.CompilerParams(collective_id=1, has_side_effects=True),
+        name="exchange",
+    )(returned)
     return pl.pallas_call(
         merge_kernel,
         out_shape=(

time: 110 us -> 62.1 us (0.56)
  waiting for transfers between devices: 60.2 us -> 0 us
  Pallas kernels: 15.7 us -> 56.8 us
  between operations: 14.1 us -> 0.66 us
  blocking collectives: 11.9 us -> 0 us
  other arithmetic: 6.45 us -> 3.5 us
    all_gather x1 -> x0, waiting for transfers between devices: 60.2 us -> none  [shards(): everyone = lax.all_gather(packed, AXES, axis=0, tiled=True)]
    pallas_call x0 -> x2, Pallas kernels: none -> 41.1 us  [the longest x1 29 us: shards(): pl.pallas_call(functools.partial(gather_kernel, split), out_shape=tuple((...]
    all_to_all x1 -> x0, blocking collectives: 11.9 us -> none  [shards(): lax.all_to_all(returned, AXES, split_axis=0, concat_axis=0, tiled=True)]
    convert_element_type x3 -> x0, other arithmetic: 1.85 us -> none  [the longest x1 0.92 us: shards(): unit_rows(query_float).astype(jnp.bfloat16)]
  transfers between devices with their start and end apart: 1 -> 0, of which waited for: 1 -> 0; matrix products, arithmetic and copies ran while one was open for 0% -> 0% of each run, Pallas kernels for 0% -> 0%
where the time goes in v2:
time: 62.1 us; the launch traced here: 61.7 us
  Pallas kernels  56.8 us (91%)
  other arithmetic  3.5 us (6%)
  local copies, waits for them, and re-layouts  0.68 us (1%)
  between operations  0.66 us (1%)
    pallas_call x1, Pallas kernels, shards(): pl.pallas_call(functools.partial(gather_kernel, split), out_shape=tuple((...  29 us
    pallas_call x1, Pallas kernels, shards(): pl.pallas_call(functools.partial(score_kernel, probes, shorts), out_shape...  13.4 us
    pallas_call x1, Pallas kernels, shards(): pl.pallas_call(exchange_kernel, out_shape=jax.ShapeDtypeStruct(returned.s...  12.1 us
    another operation x5, other arithmetic  3.5 us
    pallas_call x1, Pallas kernels, shards(): pl.pallas_call(merge_kernel, out_shape=(jax.ShapeDtypeStruct((query_rows,...  2.25 us

profile of v2, /device:TPU:0, one launch (start us, length us, event | category | flops | bytes accessed | tf_op | source)
XLA Modules:
  0.0 61.7 jit_solution(1122394069509481892)
XLA Ops:
  0.6 0.7 %convert.15 = bf16[16,16]{1,0:T(8,128)(2,1)S(1)} convert(s32[16,16]{1,0:T(8,128)} %param.9) | non-fusion elementwise | flops 256 | bytes 1536 | tf_op jit(solution)/shard_map/convert
  1.3 0.7 %convert.16 = bf16[16,16]{1,0:T(8,128)(2,1)S(1)} convert(s32[16,16]{1,0:T(8,128)} %param.10) | non-fusion elementwise | flops 256 | bytes 1536 | tf_op jit(solution)/shard_map/convert.1
  2.0 0.7 %convert.18 = bf16[16,32]{1,0:T(8,128)(2,1)S(1)} convert(s32[16,32]{1,0:T(8,128)} %param.14) | non-fusion elementwise | flops 512 | bytes 3072 | tf_op jit(solution)/shard_map/convert.3
  2.7 0.7 %convert.19 = bf16[16,32]{1,0:T(8,128)(2,1)S(1)} convert(s32[16,32]{1,0:T(8,128)} %param.15) | non-fusion elementwise | flops 512 | bytes 3072 | tf_op jit(solution)/shard_map/convert.4
  3.4 0.7 %convert.17 = bf16[16,32]{1,0:T(8,128)(2,1)S(1)} convert(s32[16,32]{1,0:T(8,128)} %dev_ref.1) | non-fusion elementwise | flops 512 | bytes 3072 | tf_op jit(solution)/shard_map/convert.2
  4.1 0.7 %concatenate.4.code_ref = bf16[16,128]{1,0:T(8,128)(2,1)} concatenate(bf16[16,16]{1,0:T(8,128)(2,1)S(1)} %convert.15, bf16[16,16]{1,0:T(8,128)(2,1)S(1)} %convert.16, bf16[16,32]{1,0:T(8,128)(2,1)S(1)} %convert.17, bf16[16,32]{1,0:T(8,128)(2,1)S(1)} %convert.18, bf16[16,32]{1,0:T(8,128)(2,1)S(1)} %convert.19), dimensions={1} | concatenate | bytes 8192 | tf_op jit(solution)/shard_map/concatenate | solution.py:280
  4.8 29.0 %gather.1 = (bf16[2,2,2,4,16,1280]{5,4,3,2,1,0:T(8,128)(2,1)}, bf16[2,2,2,4,16,1152]{5,4,3,2,1,0:T(8,128)(2,1)}) custom-call(bf16[16,2048]{1,0:T(8,128)(2,1)} %q_ref.1, bf16[16,128]{1,0:T(8,128)(2,1)} %concatenate.4.code_ref), custom_call_target="tpu_custom_call" | custom-call | tf_op jit(solution)/shard_map/gather/pallas_call | solution.py:286
  33.8 13.4 %score.1.src_ref = f32[32,8,128]{2,1,0:T(8,128)} custom-call(bf16[512,1280]{1,0:T(8,128)(2,1)} %bitcast.2, bf16[512,1152]{1,0:T(8,128)(2,1)} %bitcast.3, s32[16]{0:T(128)} %len_ref.1, bf16[16,256,2048]{2,1,0:T(8,128)(2,1)} %docs_ref.1), custom_call_target="tpu_custom_call" | custom-call | tf_op jit(solution)/shard_map/score/pallas_call | solution.py:305
  47.3 12.1 %exchange.1.got_ref = f32[32,8,128]{2,1,0:T(8,128)} custom-call(f32[32,8,128]{2,1,0:T(8,128)} %score.1.src_ref), custom_call_target="tpu_custom_call" | custom-call | tf_op jit(solution)/shard_map/exchange/pallas_call | solution.py:320
  59.4 2.3 %merge.1 = (f32[16,32]{1,0:T(8,128)}, f32[16,32]{1,0:T(8,128)}) custom-call(f32[32,8,128]{2,1,0:T(8,128)} %exchange.1.got_ref, s32[16,32]{1,0:T(8,128)} %dev_ref.1), custom_call_target="tpu_custom_call" | custom-call | tf_op jit(solution)/shard_map/merge/pallas_call | solution.py:333
